TPU v7x, 16 devices: a whole 2x2x2 slice. The times are simulated.
16 devices in a mesh: tp: 16 (over z, y, x, core).
Axes of the slice: x: 2, y: 2, z: 2, core: 2. Of those that a mesh axis runs over, the one named last changes fastest.
Arguments:
- hidden_in: bfloat16 [2, 3072, 3584], P(None, 'tp')
- lengths: int32 [2], replicated
- attn_norm: bfloat16 [2, 3584], replicated
- w_query: bfloat16 [2, 3584, 28, 128], replicated
- w_key: bfloat16 [2, 3584, 4, 128], replicated
- w_value: bfloat16 [2, 3584, 4, 128], replicated
- w_out: bfloat16 [2, 28, 128, 3584], replicated
- mlp_norm: bfloat16 [2, 3584], replicated
- w_gate: bfloat16 [2, 3584, 18944], P(None, None, 'tp')
- w_up: bfloat16 [2, 3584, 18944], P(None, None, 'tp')
- w_down: bfloat16 [2, 18944, 3584], P(None, 'tp')
- final_norm: bfloat16 [3584], replicated
Outputs:
- output: bfloat16 [2, 3072, 3584], P(None, 'tp')
All inputs are finite; a program needn't handle non-finite values.
Results may differ from a plain program's by a relative error of at most 0.02.
Values are sent between devices in bfloat16 or wider.
A program may use at most 1 GiB of HBM per device.

v0:
```python
import jax
import jax.numpy as jnp
from jax import lax
from jax.sharding import PartitionSpec as P

NORM_EPS = 1e-5
ROPE_BASE = 500000.0


def rms_norm(hidden, gain):
    h_wide = hidden.astype(jnp.float32)
    inv_rms = lax.rsqrt(jnp.mean(h_wide * h_wide, axis=-1, keepdims=True) + NORM_EPS)
    return (h_wide * inv_rms * gain.astype(jnp.float32)).astype(jnp.bfloat16)


def rope_tables(positions, head_dim):
    half_dim = head_dim // 2
    inv_freq = ROPE_BASE ** (-2.0 * jnp.arange(half_dim).astype(jnp.float32) / head_dim)
    angles = positions.astype(jnp.float32)[:, None, None] * inv_freq[None, None, :]
    return jnp.cos(angles), jnp.sin(angles)


def rotate(proj, cos_tab, sin_tab):
    half_dim = proj.shape[-1] // 2
    first = proj[..., :half_dim]
    second = proj[..., half_dim:]
    return jnp.concatenate([first * cos_tab - second * sin_tab, second * cos_tab + first * sin_tab], axis=-1)


def attend(q_rot, k_all, v_all, q_pos, lengths):
    head_dim = q_rot.shape[-1]
    key_pos = jnp.arange(k_all.shape[1])
    allowed = (key_pos[None, None, :] <= q_pos[None, :, None]) & (key_pos[None, None, :] < lengths[:, None, None])
    scores = jnp.einsum('bqkgd,bskd->bkgqs', q_rot, k_all, preferred_element_type=jnp.float32) * (head_dim ** -0.5)
    scores = jnp.where(allowed[:, None, None, :, :], scores, -1e30)
    prob_mat = jax.nn.softmax(scores, axis=-1).astype(jnp.bfloat16)
    context = jnp.einsum('bkgqs,bskd->bqkgd', prob_mat, v_all, preferred_element_type=jnp.float32)
    return context.astype(jnp.bfloat16)


def solution(mesh):
    tp_size = mesh.shape['tp']

    def device_fn(hidden_in, lengths, attn_norm, w_query, w_key, w_value, w_out, mlp_norm, w_gate, w_up, w_down, final_norm):
        batch, seq_dev, d_model = hidden_in.shape
        heads = w_query.shape[2]
        head_dim = w_query.shape[3]
        kv_heads = w_key.shape[2]
        groups = heads // kv_heads
        q_pos = lax.axis_index('tp') * seq_dev + jnp.arange(seq_dev)
        cos_tab, sin_tab = rope_tables(q_pos, head_dim)
        hidden = hidden_in
        for layer in range(w_query.shape[0]):
            normed = rms_norm(hidden, attn_norm[layer])
            q_proj = jnp.einsum('bsd,dhe->bshe', normed, w_query[layer], preferred_element_type=jnp.float32)
            k_proj = jnp.einsum('bsd,dhe->bshe', normed, w_key[layer], preferred_element_type=jnp.float32)
            v_proj = jnp.einsum('bsd,dhe->bshe', normed, w_value[layer], preferred_element_type=jnp.float32).astype(jnp.bfloat16)
            q_rot = rotate(q_proj, cos_tab, sin_tab).astype(jnp.bfloat16).reshape(batch, seq_dev, kv_heads, groups, head_dim)
            k_rot = rotate(k_proj, cos_tab, sin_tab).astype(jnp.bfloat16)
            k_all = lax.all_gather(k_rot, 'tp', axis=1, tiled=True)
            v_all = lax.all_gather(v_proj, 'tp', axis=1, tiled=True)
            context = attend(q_rot, k_all, v_all, q_pos, lengths).reshape(batch, seq_dev, heads, head_dim)
            attn_out = jnp.einsum('bshe,hed->bsd', context, w_out[layer], preferred_element_type=jnp.float32)
            hidden = (hidden.astype(jnp.float32) + attn_out).astype(jnp.bfloat16)
            normed = rms_norm(hidden, mlp_norm[layer])
            full_normed = lax.all_gather(normed, 'tp', axis=1, tiled=True)
            gate_proj = jnp.einsum('bsd,df->bsf', full_normed, w_gate[layer], preferred_element_type=jnp.float32)
            up_proj = jnp.einsum('bsd,df->bsf', full_normed, w_up[layer], preferred_element_type=jnp.float32)
            gated_act = (jax.nn.silu(gate_proj) * up_proj).astype(jnp.bfloat16)
            part_out = jnp.einsum('bsf,fd->bsd', gated_act, w_down[layer], preferred_element_type=jnp.float32).astype(jnp.bfloat16)
            part_out = part_out.reshape(batch, tp_size, seq_dev, d_model)
            received = lax.all_to_all(part_out, 'tp', 1, 1, tiled=True)
            mlp_out = jnp.sum(received, axis=1, dtype=jnp.float32)
            hidden = (hidden.astype(jnp.float32) + mlp_out).astype(jnp.bfloat16)
        return rms_norm(hidden, final_norm)

    seq_part = P(None, 'tp', None)
    in_specs = (seq_part, P(), P(), P(), P(), P(), P(), P(), P(None, None, 'tp'), P(None, None, 'tp'), P(None, 'tp', None), P())
    return jax.shard_map(device_fn, mesh=mesh, in_specs=in_specs, out_specs=seq_part, check_vma=False)
```

profile of v0, /device:TPU:0, one launch (start us, length us, event | category | flops | bytes accessed | tf_op | source)
XLA Modules:
  0.0 2216.4 jit_solution(17120288243772005391)
XLA Ops:
  29.0 15.8 fusion.22
  49.6 13.7 all-gather.9.cloned.1.call-done
  63.2 58.0 %fusion.132 = (f32[2,4,7,192]{3,2,1,0:T(8,128)S(1)}, f32[2,4,7,192,3072]{4,3,2,1,0:T(8,128)}) fusion(pred[2,192,3072]{2,1,0:T(8,128)(4,1)S(1)} %broadcast_and_fusion, bf16[2,3072,4,128]{3,1,2,0:T(8,128)(2,1)} %all-gather.9.cloned.1.call-done, bf16[2,192,4,7,64]{4,1,3,2,0:T(8,128)(2,1)} %bitcast.205, bf16[2,192,4,7,64]{4,1,3,2,0:T(8,128)(2,1)} %bitcast.204), kind=kOutput, calls=%fused_computation.149 | convolution fusion | flops 8593345536 | bytes 142387200 | tf_op jit(solution)/shard_map/sub | solution.py:36
  121.2 56.2 %fusion.102 = bf16[2,4,128,7,192]{2,4,3,1,0:T(8,128)(2,1)} fusion(f32[2,4,7,192,3072]{4,3,2,1,0:T(8,128)} %get-tuple-element.26, f32[2,4,7,192]{3,2,1,0:T(8,128)S(1)} %get-tuple-element.25, bf16[2,3072,4,128]{3,1,2,0:T(8,128)(2,1)} %all-gather.7.cloned.1.call-done), kind=kOutput, calls=%fused_computation.116 | convolution fusion | flops 8523153408 | bytes 141207552 | tf_op jit(solution)/shard_map/bkgqs,bskd->bqkgd/dot_general | solution.py:37
  177.4 16.2 fusion.80
  197.6 165.7 %all-gather.11.cloned.1.call-done = bf16[2,3072,3584]{2,1,0:T(8,128)(2,1)} async-done(((bf16[2,192,3584]{2,1,0:T(8,128)(2,1)}), bf16[2,3072,3584]{2,1,0:T(8,128)(2,1)}) %all-gather.11.cloned.1.call-update) | async-done | bytes 44040208 | tf_op jit(solution)/shard_map/all_gather | solution.py:66
  363.3 61.8 %fusion.33 = f32[2,3072,1184]{1,2,0:T(8,128)} fusion(bf16[2,3072,3584]{2,1,0:T(8,128)(2,1)} %all-gather.11.cloned.1.call-done, bf16[2,3584,1184]{1,2,0:T(8,128)(2,1)} %param.21), kind=kOutput, calls=%fused_computation.43 | convolution fusion | flops 52143587328 | bytes 81625088 | tf_op jit(solution)/shard_map/bsd,df->bsf/dot_general | solution.py:68
  425.1 65.0 %multiply_convert_fusion.1 = bf16[2,3072,1184]{1,2,0:T(8,128)(2,1)} fusion(f32[2,3072,1184]{1,2,0:T(8,128)} %fusion.33, bf16[2,3072,3584]{2,1,0:T(8,128)(2,1)} %all-gather.11.cloned.1.call-done, bf16[2,3584,1184]{1,2,0:T(8,128)(2,1)} %param.20), kind=kOutput, calls=%fused_computation.23 | convolution fusion | flops 52187234304 | bytes 96174080 | tf_op jit(solution)/shard_map/bsd,df->bsf/dot_general | solution.py:67
  490.0 65.7 %convolution_convert_fusion.1 = bf16[2,3072,3584]{2,1,0:T(8,128)(2,1)} fusion(bf16[2,3072,1184]{1,2,0:T(8,128)(2,1)} %multiply_convert_fusion.1, bf16[2,1184,3584]{2,1,0:T(8,128)(2,1)} %param.22), kind=kOutput, calls=%fused_computation.21 | convolution fusion | flops 52165607424 | bytes 67076096 | tf_op jit(solution)/shard_map/bsf,fd->bsd/dot_general | solution.py:70
  555.7 29.8 %copy.16 = bf16[2,16,192,3584]{3,2,0,1:T(8,128)(2,1)} copy(bf16[2,16,192,3584]{3,2,1,0:T(8,128)(2,1)} %bitcast.202) | data formatting | bytes 88080384 | tf_op jit(solution)/shard_map/reshape | solution.py:71
  585.5 484.2 %all_to_all.10 = bf16[2,16,192,3584]{3,2,0,1:T(8,128)(2,1)} all-to-all(bf16[2,16,192,3584]{3,2,0,1:T(8,128)(2,1)} %copy.16), channel_id=1, replica_groups=mesh['tp'=16] {'tp'}, dimensions={1} | all-to-all | bytes 88080384 | tf_op jit(solution)/shard_map/all_to_all | solution.py:72
  1069.7 17.5 convert_reduce_fusion.1
  1099.6 15.8 fusion.18
  1119.0 24.0 %all-gather.15.cloned.1.call-done = bf16[2,3072,4,128]{3,1,2,0:T(8,128)(2,1)} async-done(((bf16[2,192,4,128]{3,1,2,0:T(8,128)(2,1)}), bf16[2,3072,4,128]{3,1,2,0:T(8,128)(2,1)}) %all-gather.15.cloned.1.call-update) | async-done | bytes 6291472 | tf_op jit(solution)/shard_map/all_gather | solution.py:60
  1142.9 58.2 %fusion.137 = (f32[2,4,7,192]{3,2,1,0:T(8,128)S(1)}, f32[2,4,7,192,3072]{4,3,2,1,0:T(8,128)}) fusion(pred[2,192,3072]{2,1,0:T(8,128)(4,1)} %copy-done.14, bf16[2,3072,4,128]{3,1,2,0:T(8,128)(2,1)} %all-gather.15.cloned.1.call-done, bf16[2,192,4,7,64]{4,1,3,2,0:T(8,128)(2,1)} %bitcast.207, bf16[2,192,4,7,64]{4,1,3,2,0:T(8,128)(2,1)} %bitcast.206), kind=kOutput, calls=%fused_computation.150 | convolution fusion | flops 8593345536 | bytes 142387200 | tf_op jit(solution)/shard_map/sub | solution.py:36
  1201.2 45.0 %fusion.99 = bf16[2,4,128,7,192]{2,4,3,1,0:T(8,128)(2,1)} fusion(f32[2,4,7,192,3072]{4,3,2,1,0:T(8,128)} %get-tuple-element.30, f32[2,4,7,192]{3,2,1,0:T(8,128)S(1)} %get-tuple-element.29, bf16[2,3072,4,128]{3,1,2,0:T(8,128)(2,1)} %all-gather.13.cloned.1.call-done), kind=kOutput, calls=%fused_computation.115 | convolution fusion | flops 8523153408 | bytes 141207552 | tf_op jit(solution)/shard_map/bkgqs,bskd->bqkgd/dot_general | solution.py:37
  1246.2 16.3 fusion.87
  1266.4 165.7 %all-gather.17.cloned.1.call-done = bf16[2,3072,3584]{2,1,0:T(8,128)(2,1)} async-done(((bf16[2,192,3584]{2,1,0:T(8,128)(2,1)}), bf16[2,3072,3584]{2,1,0:T(8,128)(2,1)}) %all-gather.17.cloned.1.call-update) | async-done | bytes 44040208 | tf_op jit(solution)/shard_map/all_gather | solution.py:66
  1432.1 61.8 %fusion.29 = f32[2,3072,1184]{1,2,0:T(8,128)} fusion(bf16[2,3072,3584]{2,1,0:T(8,128)(2,1)} %all-gather.17.cloned.1.call-done, bf16[2,3584,1184]{1,2,0:T(8,128)(2,1)} %param.21), kind=kOutput, calls=%fused_computation.39 | convolution fusion | flops 52143587328 | bytes 81625088 | tf_op jit(solution)/shard_map/bsd,df->bsf/dot_general | solution.py:68
  1493.9 65.4 %multiply_convert_fusion = bf16[2,3072,1184]{1,2,0:T(8,128)(2,1)} fusion(f32[2,3072,1184]{1,2,0:T(8,128)} %fusion.29, bf16[2,3072,3584]{2,1,0:T(8,128)(2,1)} %all-gather.17.cloned.1.call-done, bf16[2,3584,1184]{1,2,0:T(8,128)(2,1)} %param.20), kind=kOutput, calls=%fused_computation.22 | convolution fusion | flops 52187234304 | bytes 96174080 | tf_op jit(solution)/shard_map/bsd,df->bsf/dot_general | solution.py:67
  1559.3 65.3 %convolution_convert_fusion = bf16[2,3072,3584]{2,1,0:T(8,128)(2,1)} fusion(bf16[2,3072,1184]{1,2,0:T(8,128)(2,1)} %multiply_convert_fusion, bf16[2,1184,3584]{2,1,0:T(8,128)(2,1)} %param.22), kind=kOutput, calls=%fused_computation.20 | convolution fusion | flops 52165607424 | bytes 67076096 | tf_op jit(solution)/shard_map/bsf,fd->bsd/dot_general | solution.py:70
  1624.6 29.8 %copy.18 = bf16[2,16,192,3584]{3,2,0,1:T(8,128)(2,1)} copy(bf16[2,16,192,3584]{3,2,1,0:T(8,128)(2,1)} %bitcast.203) | data formatting | bytes 88080384 | tf_op jit(solution)/shard_map/reshape | solution.py:71
  1659.8 525.3 %all-to-all-done.1 = bf16[2,16,192,3584]{3,2,0,1:T(8,128)(2,1)} async-done(((bf16[2,16,192,3584]{3,2,0,1:T(8,128)(2,1)}), bf16[2,16,192,3584]{3,2,0,1:T(8,128)(2,1)}, u32[]{:S(2)}, u32[]{:S(2)}) %all-to-all-start.1) | async-done | bytes 44040224 | tf_op jit(solution)/shard_map/all_to_all | solution.py:72
  2185.1 17.3 convert_reduce_fusion
  (93 shorter events, 63.1 us)
Async XLA Ops:
  6.5 56.7 %all-gather.9.cloned.1.call-start = ((), (), s32[]{:S(2)}) async-start(), calls=%async_computation.3 | async-start | bytes 6684672 | tf_op jit(solution)/shard_map/all_gather | solution.py:60
  7.1 6.6 copy-start.17
  7.1 7.2 copy-start.6
  15.0 10.0 copy-start.21
  15.4 30.1 %copy-start.10 = (f32[192,64]{1,0:T(8,128)}, f32[192,64]{1,0:T(8,128)S(1)}, u32[]{:S(2)}) copy-start(f32[192,64]{1,0:T(8,128)S(1)} %get-tuple-element.23) | copy-start | bytes 147460
  15.4 30.1 %copy-start.12 = (f32[192,64]{1,0:T(8,128)}, f32[192,64]{1,0:T(8,128)S(1)}, u32[]{:S(2)}) copy-start(f32[192,64]{1,0:T(8,128)S(1)} %get-tuple-element.24) | copy-start | bytes 147460
  18.5 102.7 %all-gather.7.cloned.1.call-start = ((), (), s32[]{:S(2)}) async-start(), calls=%async_computation.2 | async-start | bytes 6684672 | tf_op jit(solution)/shard_map/all_gather | solution.py:61
  27.4 335.9 %all-gather.11.cloned.1.call-start = ((), (), s32[]{:S(2)}) async-start(), calls=%async_computation.4 | async-start | bytes 46792704 | tf_op jit(solution)/shard_map/all_gather | solution.py:66
  28.9 15.9 copy-start.18
  49.5 71.6 %copy-start.14 = (pred[2,192,3072]{2,1,0:T(8,128)(4,1)}, pred[2,192,3072]{2,1,0:T(8,128)(4,1)S(1)}, u32[]{:S(2)}) copy-start(pred[2,192,3072]{2,1,0:T(8,128)(4,1)S(1)} %broadcast_and_fusion) | copy-start | bytes 3538948
  121.2 56.2 %copy-start.7 = (bf16[2,192,3584]{2,1,0:T(8,128)(2,1)S(1)}, bf16[2,192,3584]{2,1,0:T(8,128)(2,1)}, u32[]{:S(2)}) copy-start(bf16[2,192,3584]{2,1,0:T(8,128)(2,1)} %param.12) | copy-start | bytes 8257540
  177.4 17.8 copy-start.16
  197.6 945.4 %all-gather.15.cloned.1.call-start = ((), (), s32[]{:S(2)}) async-start(), calls=%async_computation.6 | async-start | bytes 6684672 | tf_op jit(solution)/shard_map/all_gather | solution.py:60
  1069.7 17.5 copy-start.4
  1087.2 3.7 copy-start.5
  1087.2 3.8 copy-start.19
  1094.0 107.1 %all-gather.13.cloned.1.call-start = ((), (), s32[]{:S(2)}) async-start(), calls=%async_computation.5 | async-start | bytes 6684672 | tf_op jit(solution)/shard_map/all_gather | solution.py:61
  1099.5 332.6 %all-gather.17.cloned.1.call-start = ((), (), s32[]{:S(2)}) async-start(), calls=%async_computation.7 | async-start | bytes 46792704 | tf_op jit(solution)/shard_map/all_gather | solution.py:66
  1201.2 45.0 %copy-start.9 = (bf16[2,192,3584]{2,1,0:T(8,128)(2,1)S(1)}, bf16[2,192,3584]{2,1,0:T(8,128)(2,1)}, u32[]{:S(2)}) copy-start(bf16[2,192,3584]{2,1,0:T(8,128)(2,1)} %copy-done.8) | copy-start | bytes 8257540
  1246.2 17.8 copy-start.15
  1654.4 5.4 copy-start.20
  1654.4 530.7 %all-to-all-start.1 = ((bf16[2,16,192,3584]{3,2,0,1:T(8,128)(2,1)}), bf16[2,16,192,3584]{3,2,0,1:T(8,128)(2,1)}, u32[]{:S(2)}, u32[]{:S(2)}) async-start(bf16[2,16,192,3584]{3,2,0,1:T(8,128)(2,1)} %copy.18), calls=%async_computation.1 | async-start | bytes 88080384 | tf_op jit(solution)/shard_map/all_to_all | solution.py:72
  1659.8 542.6 %copy-start.2 = (bf16[2,192,3584]{2,1,0:T(8,128)(2,1)S(1)}, bf16[2,192,3584]{2,1,0:T(8,128)(2,1)}, u32[]{:S(2)}) copy-start(bf16[2,192,3584]{2,1,0:T(8,128)(2,1)} %copy-done.1) | copy-start | bytes 8257540
  2202.4 4.2 copy-start
  (6 other events, 11.0 us)
Sparse Core Ops, SparseCore 0:
  18.6 44.5 all-gather.8
  65.5 41.7 all-gather.6
  197.7 165.5 all-gather.10
  1094.1 48.7 all-gather.14
  1145.0 41.7 all-gather.12
  1266.5 165.5 all-gather.16
where the time goes:
time: 2220 us
  waiting for transfers between devices  894 us (40%)
  matrix products  677 us (30%)
  blocking collectives  484 us (22%)
  local copies, waits for them, and re-layouts  76.3 us (3%)
  other arithmetic  63.9 us (3%)
    all_to_all x1, waiting for transfers between devices, device_fn(): received = lax.all_to_all(part_out, 'tp', 1, 1, tiled=True)  525 us
    all_to_all x1, blocking collectives, device_fn(): received = lax.all_to_all(part_out, 'tp', 1, 1, tiled=True)  484 us
    all_gather x2, waiting for transfers between devices, device_fn(): full_normed = lax.all_gather(normed, 'tp', axis=1, tiled=True)  331 us
    dot_general x2, matrix products, device_fn(): jnp.einsum('bsf,fd->bsd', gated_act, w_down[layer], preferred_element_typ...  131 us
    dot_general x2, matrix products, device_fn(): jnp.einsum('bsd,df->bsf', full_normed, w_gate[layer], preferred_element_t...  130 us
    dot_general x2, matrix products, device_fn(): jnp.einsum('bsd,df->bsf', full_normed, w_up[layer], preferred_element_typ...  124 us
    sub x2, matrix products, attend(): prob_mat = jax.nn.softmax(scores, axis=-1).astype(jnp.bfloat16)  116 us
    dot_general x2, matrix products, attend(): jnp.einsum('bkgqs,bskd->bqkgd', prob_mat, v_all, preferred_element_type=j...  101 us
  transfers between devices with their start and end apart: 7, of which 5 were waited for; matrix products, arithmetic and copies ran while one was open for 8% of the time, Pallas kernels for 0%

commit v1 on v0

--- a/solution.py
+++ b/solution.py
@@ -67,10 +67,9 @@
             gate_proj = jnp.einsum('bsd,df->bsf', full_normed, w_gate[layer], preferred_element_type=jnp.float32)
             up_proj = jnp.einsum('bsd,df->bsf', full_normed, w_up[layer], preferred_element_type=jnp.float32)
             gated_act = (jax.nn.silu(gate_proj) * up_proj).astype(jnp.bfloat16)
-            part_out = jnp.einsum('bsf,fd->bsd', gated_act, w_down[layer], preferred_element_type=jnp.float32).astype(jnp.bfloat16)
-            part_out = part_out.reshape(batch, tp_size, seq_dev, d_model)
-            received = lax.all_to_all(part_out, 'tp', 1, 1, tiled=True)
-            mlp_out = jnp.sum(received, axis=1, dtype=jnp.float32)
+            part_out = jnp.einsum('bsf,fd->bsd', gated_act, w_down[layer], preferred_element_type=jnp.float32)
+            part_out = lax.reduce_precision(part_out, 8, 7)
+            mlp_out = lax.psum_scatter(part_out, 'tp', scatter_dimension=1, tiled=True)
             hidden = (hidden.astype(jnp.float32) + mlp_out).astype(jnp.bfloat16)
         return rms_norm(hidden, final_norm)
 

time: 2220 us -> 1950 us (0.88)
  blocking collectives: 484 us -> 0 us
  waiting for transfers between devices: 894 us -> 1210 us
  local copies, waits for them, and re-layouts: 76.3 us -> 17.5 us
  other arithmetic: 63.9 us -> 29.2 us
    reduce_scatter x0 -> x2, waiting for transfers between devices: none -> 845 us  [device_fn(): mlp_out = lax.psum_scatter(part_out, 'tp', scatter_dimension=1, tiled=True)]
    all_to_all x1 -> x0, waiting for transfers between devices: 525 us -> none  [device_fn(): received = lax.all_to_all(part_out, 'tp', 1, 1, tiled=True)]
    all_to_all x1 -> x0, blocking collectives: 484 us -> none  [device_fn(): received = lax.all_to_all(part_out, 'tp', 1, 1, tiled=True)]
    reshape x2 -> x0, local copies, waits for them, and re-layouts: 59.5 us -> none  [device_fn(): part_out = part_out.reshape(batch, tp_size, seq_dev, d_model)]
    reduce_sum x2 -> x0, other arithmetic: 34.7 us -> none  [device_fn(): mlp_out = jnp.sum(received, axis=1, dtype=jnp.float32)]
  transfers between devices with their start and end apart: 7 -> 8, of which waited for: 5 -> 6; matrix products, arithmetic and copies ran while one was open for 8% -> 9% of each run, Pallas kernels for 0% -> 0%
where the time goes in v1:
time: 1950 us; the launch traced here: 1940 us
  waiting for transfers between devices  1210 us (62%)
  matrix products  672 us (34%)
  other arithmetic  29.2 us (1%)
    reduce_scatter x2, waiting for transfers between devices, device_fn(): mlp_out = lax.psum_scatter(part_out, 'tp', scatter_dimension=1, tiled=True)  845 us
    all_gather x2, waiting for transfers between devices, device_fn(): full_normed = lax.all_gather(normed, 'tp', axis=1, tiled=True)  331 us
    dot_general x2, matrix products, device_fn(): jnp.einsum('bsf,fd->bsd', gated_act, w_down[layer], preferred_element_typ...  137 us
    dot_general x2, matrix products, device_fn(): jnp.einsum('bsd,df->bsf', full_normed, w_gate[layer], preferred_element_t...  130 us
    dot_general x2, matrix products, device_fn(): jnp.einsum('bsd,df->bsf', full_normed, w_up[layer], preferred_element_typ...  124 us
    sub x2, matrix products, attend(): prob_mat = jax.nn.softmax(scores, axis=-1).astype(jnp.bfloat16)  116 us
    dot_general x2, matrix products, attend(): jnp.einsum('bkgqs,bskd->bqkgd', prob_mat, v_all, preferred_element_type=j...  90.3 us
  transfers between devices with their start and end apart: 8, of which 6 were waited for; matrix products, arithmetic and copies ran while one was open for 9% of the time, Pallas kernels for 0%

profile of v1, /device:TPU:0, one launch (start us, length us, event | category | flops | bytes accessed | tf_op | source)
XLA Modules:
  0.0 1941.3 jit_solution(3885445098351032527)
XLA Ops:
  7.1 6.6 fusion.131
  18.5 6.4 slice_bitcast_fusion
  28.8 15.8 fusion.22
  49.4 13.8 all-gather.9.cloned.1.call-done
  63.2 58.0 %fusion.132 = (f32[2,4,7,192]{3,2,1,0:T(8,128)S(1)}, f32[2,4,7,192,3072]{4,3,2,1,0:T(8,128)}) fusion(pred[2,192,3072]{2,1,0:T(8,128)(4,1)S(1)} %broadcast_and_fusion, bf16[2,3072,4,128]{3,1,2,0:T(8,128)(2,1)} %all-gather.9.cloned.1.call-done, bf16[2,192,4,7,64]{4,1,3,2,0:T(8,128)(2,1)} %bitcast.201, bf16[2,192,4,7,64]{4,1,3,2,0:T(8,128)(2,1)} %bitcast.200), kind=kOutput, calls=%fused_computation.147 | convolution fusion | flops 8593345536 | bytes 142387200 | tf_op jit(solution)/shard_map/sub | solution.py:36
  121.2 45.3 %fusion.102 = bf16[2,4,128,7,192]{2,4,3,1,0:T(8,128)(2,1)} fusion(f32[2,4,7,192,3072]{4,3,2,1,0:T(8,128)} %get-tuple-element.26, f32[2,4,7,192]{3,2,1,0:T(8,128)S(1)} %get-tuple-element.25, bf16[2,3072,4,128]{3,1,2,0:T(8,128)(2,1)} %all-gather.7.cloned.1.call-done), kind=kOutput, calls=%fused_computation.114 | convolution fusion | flops 8523153408 | bytes 141207552 | tf_op jit(solution)/shard_map/bkgqs,bskd->bqkgd/dot_general | solution.py:37
  166.5 16.3 fusion.80
  186.9 165.7 %all-gather.11.cloned.1.call-done = bf16[2,3072,3584]{2,1,0:T(8,128)(2,1)} async-done(((bf16[2,192,3584]{2,1,0:T(8,128)(2,1)}), bf16[2,3072,3584]{2,1,0:T(8,128)(2,1)}) %all-gather.11.cloned.1.call-update) | async-done | bytes 44040208 | tf_op jit(solution)/shard_map/all_gather | solution.py:66
  352.5 61.9 %fusion.33 = f32[2,3072,1184]{1,2,0:T(8,128)} fusion(bf16[2,3072,3584]{2,1,0:T(8,128)(2,1)} %all-gather.11.cloned.1.call-done, bf16[2,3584,1184]{1,2,0:T(8,128)(2,1)} %param.21), kind=kOutput, calls=%fused_computation.41 | convolution fusion | flops 52143587328 | bytes 81625088 | tf_op jit(solution)/shard_map/bsd,df->bsf/dot_general | solution.py:68
  414.4 65.0 %multiply_convert_fusion.1 = bf16[2,3072,1184]{1,2,0:T(8,128)(2,1)} fusion(f32[2,3072,1184]{1,2,0:T(8,128)} %fusion.33, bf16[2,3072,3584]{2,1,0:T(8,128)(2,1)} %all-gather.11.cloned.1.call-done, bf16[2,3584,1184]{1,2,0:T(8,128)(2,1)} %param.20), kind=kOutput, calls=%fused_computation.21 | convolution fusion | flops 52187234304 | bytes 96174080 | tf_op jit(solution)/shard_map/bsd,df->bsf/dot_general | solution.py:67
  479.3 68.6 %convolution_reduce-precision_fusion.1 = f32[2,3072,3584]{2,1,0:T(8,128)} fusion(bf16[2,3072,1184]{1,2,0:T(8,128)(2,1)} %multiply_convert_fusion.1, bf16[2,1184,3584]{2,1,0:T(8,128)(2,1)} %param.22), kind=kOutput, calls=%fused_computation.19 | convolution fusion | flops 52165607424 | bytes 111116288 | tf_op jit(solution)/shard_map/bsf,fd->bsd/dot_general | solution.py:70
  548.0 423.0 %reduce-scatter.3.cloned.1.call-done = f32[2,192,3584]{2,1,0:T(8,128)} async-done(((f32[2,3072,3584]{2,1,0:T(8,128)}), f32[2,192,3584]{2,1,0:T(8,128)}) %reduce-scatter.3.cloned.1.call-update) | async-done | bytes 5505040 | tf_op jit(solution)/shard_map/reduce_scatter | solution.py:72
  971.0 3.7 fusion.84
  977.9 5.3 fusion.108
  983.6 15.8 fusion.18
  1003.0 16.8 all-gather.15.cloned.1.call-done
  1019.8 58.2 %fusion.137 = (f32[2,4,7,192]{3,2,1,0:T(8,128)S(1)}, f32[2,4,7,192,3072]{4,3,2,1,0:T(8,128)}) fusion(pred[2,192,3072]{2,1,0:T(8,128)(4,1)} %copy-done.14, bf16[2,3072,4,128]{3,1,2,0:T(8,128)(2,1)} %all-gather.15.cloned.1.call-done, bf16[2,192,4,7,64]{4,1,3,2,0:T(8,128)(2,1)} %bitcast.203, bf16[2,192,4,7,64]{4,1,3,2,0:T(8,128)(2,1)} %bitcast.202), kind=kOutput, calls=%fused_computation.148 | convolution fusion | flops 8593345536 | bytes 142387200 | tf_op jit(solution)/shard_map/sub | solution.py:36
  1078.0 45.0 %fusion.99 = bf16[2,4,128,7,192]{2,4,3,1,0:T(8,128)(2,1)} fusion(f32[2,4,7,192,3072]{4,3,2,1,0:T(8,128)} %get-tuple-element.30, f32[2,4,7,192]{3,2,1,0:T(8,128)S(1)} %get-tuple-element.29, bf16[2,3072,4,128]{3,1,2,0:T(8,128)(2,1)} %all-gather.13.cloned.1.call-done), kind=kOutput, calls=%fused_computation.113 | convolution fusion | flops 8523153408 | bytes 141207552 | tf_op jit(solution)/shard_map/bkgqs,bskd->bqkgd/dot_general | solution.py:37
  1123.0 16.2 fusion.87
  1143.3 165.7 %all-gather.17.cloned.1.call-done = bf16[2,3072,3584]{2,1,0:T(8,128)(2,1)} async-done(((bf16[2,192,3584]{2,1,0:T(8,128)(2,1)}), bf16[2,3072,3584]{2,1,0:T(8,128)(2,1)}) %all-gather.17.cloned.1.call-update) | async-done | bytes 44040208 | tf_op jit(solution)/shard_map/all_gather | solution.py:66
  1308.9 61.9 %fusion.29 = f32[2,3072,1184]{1,2,0:T(8,128)} fusion(bf16[2,3072,3584]{2,1,0:T(8,128)(2,1)} %all-gather.17.cloned.1.call-done, bf16[2,3584,1184]{1,2,0:T(8,128)(2,1)} %param.21), kind=kOutput, calls=%fused_computation.37 | convolution fusion | flops 52143587328 | bytes 81625088 | tf_op jit(solution)/shard_map/bsd,df->bsf/dot_general | solution.py:68
  1370.8 65.0 %multiply_convert_fusion = bf16[2,3072,1184]{1,2,0:T(8,128)(2,1)} fusion(f32[2,3072,1184]{1,2,0:T(8,128)} %fusion.29, bf16[2,3072,3584]{2,1,0:T(8,128)(2,1)} %all-gather.17.cloned.1.call-done, bf16[2,3584,1184]{1,2,0:T(8,128)(2,1)} %param.20), kind=kOutput, calls=%fused_computation.20 | convolution fusion | flops 52187234304 | bytes 96174080 | tf_op jit(solution)/shard_map/bsd,df->bsf/dot_general | solution.py:67
  1435.7 68.5 %convolution_reduce-precision_fusion = f32[2,3072,3584]{2,1,0:T(8,128)} fusion(bf16[2,3072,1184]{1,2,0:T(8,128)(2,1)} %multiply_convert_fusion, bf16[2,1184,3584]{2,1,0:T(8,128)(2,1)} %param.22), kind=kOutput, calls=%fused_computation.18 | convolution fusion | flops 52165607424 | bytes 111116288 | tf_op jit(solution)/shard_map/bsf,fd->bsd/dot_general | solution.py:70
  1504.9 422.3 %reduce-scatter.5.cloned.1.call-done = f32[2,192,3584]{2,1,0:T(8,128)} async-done(((f32[2,3072,3584]{2,1,0:T(8,128)}), f32[2,192,3584]{2,1,0:T(8,128)}) %reduce-scatter.5.cloned.1.call-update) | async-done | bytes 5505040 | tf_op jit(solution)/shard_map/reduce_scatter | solution.py:72
  (92 shorter events, 36.6 us)
Async XLA Ops:
  6.5 56.7 %all-gather.9.cloned.1.call-start = ((), (), s32[]{:S(2)}) async-start(), calls=%async_computation.3 | async-start | bytes 6684672 | tf_op jit(solution)/shard_map/all_gather | solution.py:60
  7.1 6.6 copy-start.17
  7.1 7.2 copy-start.6
  15.0 10.0 copy-start.21
  15.4 29.9 %copy-start.10 = (f32[192,64]{1,0:T(8,128)}, f32[192,64]{1,0:T(8,128)S(1)}, u32[]{:S(2)}) copy-start(f32[192,64]{1,0:T(8,128)S(1)} %get-tuple-element.23) | copy-start | bytes 147460
  15.4 29.9 %copy-start.12 = (f32[192,64]{1,0:T(8,128)}, f32[192,64]{1,0:T(8,128)S(1)}, u32[]{:S(2)}) copy-start(f32[192,64]{1,0:T(8,128)S(1)} %get-tuple-element.24) | copy-start | bytes 147460
  18.5 102.7 %all-gather.7.cloned.1.call-start = ((), (), s32[]{:S(2)}) async-start(), calls=%async_computation.2 | async-start | bytes 6684672 | tf_op jit(solution)/shard_map/all_gather | solution.py:61
  27.4 325.1 %all-gather.11.cloned.1.call-start = ((), (), s32[]{:S(2)}) async-start(), calls=%async_computation.4 | async-start | bytes 46792704 | tf_op jit(solution)/shard_map/all_gather | solution.py:66
  28.8 15.9 copy-start.18
  49.4 71.8 %copy-start.14 = (pred[2,192,3072]{2,1,0:T(8,128)(4,1)}, pred[2,192,3072]{2,1,0:T(8,128)(4,1)S(1)}, u32[]{:S(2)}) copy-start(pred[2,192,3072]{2,1,0:T(8,128)(4,1)S(1)} %broadcast_and_fusion) | copy-start | bytes 3538948
  121.2 45.3 %copy-start.7 = (bf16[2,192,3584]{2,1,0:T(8,128)(2,1)S(1)}, bf16[2,192,3584]{2,1,0:T(8,128)(2,1)}, u32[]{:S(2)}) copy-start(bf16[2,192,3584]{2,1,0:T(8,128)(2,1)} %param.12) | copy-start | bytes 8257540
  166.5 17.9 copy-start.16
  186.8 784.2 %reduce-scatter.3.cloned.1.call-start = ((), (), s32[]{:S(2)}) async-start(), calls=%async_computation.5 | async-start | bytes 93585408 | tf_op jit(solution)/shard_map/reduce_scatter | solution.py:72
  547.9 423.0 %copy-start.4 = (bf16[2,192,3584]{2,1,0:T(8,128)(2,1)S(1)}, bf16[2,192,3584]{2,1,0:T(8,128)(2,1)}, u32[]{:S(2)}) copy-start(bf16[2,192,3584]{2,1,0:T(8,128)(2,1)} %copy-done.3) | copy-start | bytes 8257540
  548.0 426.8 %copy-start.19 = (f32[3584]{0:T(1024)S(1)}, f32[3584]{0:T(1024)}, u32[]{:S(2)}) copy-start(f32[3584]{0:T(1024)} %get-tuple-element.7) | copy-start | bytes 43012
  548.0 471.8 %all-gather.15.cloned.1.call-start = ((), (), s32[]{:S(2)}) async-start(), calls=%async_computation.7 | async-start | bytes 6684672 | tf_op jit(solution)/shard_map/all_gather | solution.py:60
  971.0 3.8 copy-start.5
  977.8 100.2 %all-gather.13.cloned.1.call-start = ((), (), s32[]{:S(2)}) async-start(), calls=%async_computation.6 | async-start | bytes 6684672 | tf_op jit(solution)/shard_map/all_gather | solution.py:61
  983.1 325.8 %all-gather.17.cloned.1.call-start = ((), (), s32[]{:S(2)}) async-start(), calls=%async_computation.8 | async-start | bytes 46792704 | tf_op jit(solution)/shard_map/all_gather | solution.py:66
  1078.0 45.0 %copy-start.9 = (bf16[2,192,3584]{2,1,0:T(8,128)(2,1)S(1)}, bf16[2,192,3584]{2,1,0:T(8,128)(2,1)}, u32[]{:S(2)}) copy-start(bf16[2,192,3584]{2,1,0:T(8,128)(2,1)} %copy-done.8) | copy-start | bytes 8257540
  1123.0 17.8 copy-start.15
  1143.2 784.1 %reduce-scatter.5.cloned.1.call-start = ((), (), s32[]{:S(2)}) async-start(), calls=%async_computation.9 | async-start | bytes 93585408 | tf_op jit(solution)/shard_map/reduce_scatter | solution.py:72
  1504.2 423.0 %copy-start.1 = (bf16[2,192,3584]{2,1,0:T(8,128)(2,1)S(1)}, bf16[2,192,3584]{2,1,0:T(8,128)(2,1)}, u32[]{:S(2)}) copy-start(bf16[2,192,3584]{2,1,0:T(8,128)(2,1)} %copy-done) | copy-start | bytes 8257540
  1927.3 4.2 copy-start.2
  (7 other events, 11.5 us)
Sparse Core Ops, SparseCore 0:
  18.6 44.6 all-gather.8
  65.5 41.7 all-gather.6
  186.9 165.5 all-gather.10
  548.1 422.8 reduce-scatter.2
  977.9 41.7 all-gather.14
  1021.9 41.7 all-gather.12
  1143.3 165.5 all-gather.16
  1504.4 422.8 reduce-scatter.4

commit v2 on v1

v2 whole, which is shorter than its diff:
```python
import jax
import jax.numpy as jnp
from jax import lax
from jax.sharding import PartitionSpec as P

NORM_EPS = 1e-5
ROPE_BASE = 500000.0
AXIS_BIT = {'z': 8, 'y': 4, 'x': 2, 'core': 1}
COLOURS = (('x', 'y', 'z'), ('y', 'z', 'x'), ('z', 'x', 'y'))


def rms_norm(hidden, gain):
    h_wide = hidden.astype(jnp.float32)
    inv_rms = lax.rsqrt(jnp.mean(h_wide * h_wide, axis=-1, keepdims=True) + NORM_EPS)
    return (h_wide * inv_rms * gain.astype(jnp.float32)).astype(jnp.bfloat16)


def rope_tables(positions, head_dim):
    half_dim = head_dim // 2
    inv_freq = ROPE_BASE ** (-2.0 * jnp.arange(half_dim).astype(jnp.float32) / head_dim)
    angles = positions.astype(jnp.float32)[:, None, None] * inv_freq[None, None, :]
    return jnp.cos(angles), jnp.sin(angles)


def rotate(proj, cos_tab, sin_tab):
    half_dim = proj.shape[-1] // 2
    first = proj[..., :half_dim]
    second = proj[..., half_dim:]
    return jnp.concatenate([first * cos_tab - second * sin_tab, second * cos_tab + first * sin_tab], axis=-1)


def attend(q_rot, k_all, v_all, q_pos, length):
    head_dim = q_rot.shape[-1]
    key_pos = jnp.arange(k_all.shape[0])
    allowed = (key_pos[None, :] <= q_pos[:, None]) & (key_pos[None, :] < length)
    scores = jnp.einsum('qkgd,skd->kgqs', q_rot, k_all, preferred_element_type=jnp.float32) * (head_dim ** -0.5)
    scores = jnp.where(allowed[None, None, :, :], scores, -1e30)
    prob_mat = jax.nn.softmax(scores, axis=-1).astype(jnp.bfloat16)
    context = jnp.einsum('kgqs,skd->qkgd', prob_mat, v_all, preferred_element_type=jnp.float32)
    return context.astype(jnp.bfloat16)


def solution(mesh):
    tp_size = mesh.shape['tp']

    def swap(arr, axis):
        bit = AXIS_BIT[axis]
        return lax.ppermute(arr, 'tp', [(i, i ^ bit) for i in range(tp_size)])

    def device_fn(hidden_in, lengths, attn_norm, w_query, w_key, w_value, w_out, mlp_norm, w_gate, w_up, w_down, final_norm):
        batch, seq_dev, d_model = hidden_in.shape
        heads = w_query.shape[2]
        head_dim = w_query.shape[3]
        kv_heads = w_key.shape[2]
        groups = heads // kv_heads
        me = lax.axis_index('tp')
        mine = {name: (me // bit) % 2 for name, bit in AXIS_BIT.items()}
        q_pos = me * seq_dev + jnp.arange(seq_dev)
        cos_tab, sin_tab = rope_tables(q_pos, head_dim)

        def pick(arr, names, axis, side):
            dim = names.index(axis)
            return lax.dynamic_index_in_dim(arr, side, dim, keepdims=False), [n for n in names if n != axis]

        def reduce_scatter(part):
            part = part.reshape(2, 2, 2, 2, seq_dev, d_model)
            names = ['z', 'y', 'x', 'core']
            away, rest = pick(part, names, 'core', 1 - mine['core'])
            own, rest = pick(part, names, 'core', mine['core'])
            got = swap(away, 'core')
            third = seq_dev // 3
            sums = []
            for c in range(3):
                rows = slice(c * third, (c + 1) * third)
                sums.append(own[..., rows, :].astype(jnp.float32) + got[..., rows, :].astype(jnp.float32))
            left = [list(rest) for _ in range(3)]
            for phase in range(3):
                sent = []
                for c in range(3):
                    axis = COLOURS[c][phase]
                    send, _ = pick(sums[c], left[c], axis, 1 - mine[axis])
                    sent.append(swap(send, axis))
                for c in range(3):
                    axis = COLOURS[c][phase]
                    keep, left[c] = pick(sums[c], left[c], axis, mine[axis])
                    sums[c] = keep + sent[c]
            return jnp.concatenate(sums, axis=0)

        hidden = [hidden_in[b] for b in range(batch)]
        for layer in range(w_query.shape[0]):
            q_rots, kv_alls, zs, parts = [], [], [], []
            for b in range(batch):
                normed = rms_norm(hidden[b], attn_norm[layer])
                k_proj = jnp.einsum('sd,dhe->she', normed, w_key[layer], preferred_element_type=jnp.float32)
                v_proj = jnp.einsum('sd,dhe->she', normed, w_value[layer], preferred_element_type=jnp.float32).astype(jnp.bfloat16)
                k_rot = rotate(k_proj, cos_tab, sin_tab).astype(jnp.bfloat16)
                kv_alls.append(lax.all_gather(jnp.concatenate([k_rot, v_proj], axis=1), 'tp', axis=0, tiled=True))
                q_proj = jnp.einsum('sd,dhe->she', normed, w_query[layer], preferred_element_type=jnp.float32)
                q_rots.append(rotate(q_proj, cos_tab, sin_tab).astype(jnp.bfloat16).reshape(seq_dev, kv_heads, groups, head_dim))
            for b in range(batch):
                k_all, v_all = kv_alls[b][:, :kv_heads], kv_alls[b][:, kv_heads:]
                context = attend(q_rots[b], k_all, v_all, q_pos, lengths[b]).reshape(seq_dev, heads, head_dim)
                attn_out = jnp.einsum('she,hed->sd', context, w_out[layer], preferred_element_type=jnp.float32)
                hidden[b] = (hidden[b].astype(jnp.float32) + attn_out).astype(jnp.bfloat16)
                normed = rms_norm(hidden[b], mlp_norm[layer])
                zs.append(lax.all_gather(normed, 'tp', axis=0, tiled=True))
            for b in range(batch):
                gate_proj = jnp.einsum('sd,df->sf', zs[b], w_gate[layer], preferred_element_type=jnp.float32)
                up_proj = jnp.einsum('sd,df->sf', zs[b], w_up[layer], preferred_element_type=jnp.float32)
                gated_act = (jax.nn.silu(gate_proj) * up_proj).astype(jnp.bfloat16)
                parts.append(jnp.einsum('sf,fd->sd', gated_act, w_down[layer], preferred_element_type=jnp.float32).astype(jnp.bfloat16))
            for b in range(batch):
                mlp_out = reduce_scatter(parts[b])
                hidden[b] = (hidden[b].astype(jnp.float32) + mlp_out).astype(jnp.bfloat16)
        return jnp.stack([rms_norm(hidden[b], final_norm) for b in range(batch)])

    seq_part = P(None, 'tp', None)
    in_specs = (seq_part, P(), P(), P(), P(), P(), P(), P(), P(None, None, 'tp'), P(None, None, 'tp'), P(None, 'tp', None), P())
    return jax.shard_map(device_fn, mesh=mesh, in_specs=in_specs, out_specs=seq_part, check_vma=False)
```

time: 1950 us -> 1910 us (0.979)
  waiting for transfers between devices: 1210 us -> 831 us
  local copies, waits for them, and re-layouts: 17.5 us -> 142 us
  other arithmetic: 29.2 us -> 123 us
  matrix products: 672 us -> 754 us
  starting transfers between devices: 0.88 us -> 44.2 us
    reduce_scatter x2 -> x0, waiting for transfers between devices: 845 us -> none  [device_fn(): mlp_out = lax.psum_scatter(part_out, 'tp', scatter_dimension=1, tiled=True)]
    ppermute x0 -> x40, waiting for transfers between devices: none -> 509 us  [swap(): return lax.ppermute(arr, 'tp', [(i, i ^ bit) for i in range(tp_size)])]
    add x1 -> x41, other arithmetic: 0.59 us -> 90.4 us  [the longest x4 50.3 us: reduce_scatter(): own[..., rows, :].astype(jnp.float32)]
    dot_general x16 -> x32, matrix products: 556 us -> 625 us  [the longest x4 144 us: device_fn(): jnp.einsum('sf,fd->sd', gated_act, w_down[layer], preferred_element_type=...]
    squeeze x1 -> x32, local copies, waits for them, and re-layouts: 6.44 us -> 72.6 us  [pick(): lax.dynamic_index_in_dim(arr, side, dim, keepdims=False)]
    ppermute x0 -> x40, starting transfers between devices: none -> 43.4 us  [swap(): return lax.ppermute(arr, 'tp', [(i, i ^ bit) for i in range(tp_size)])]
    all_gather x6 -> x8, waiting for transfers between devices: 362 us -> 321 us  [the longest x4 279 us: device_fn(): zs.append(lax.all_gather(normed, 'tp', axis=0, tiled=True))]
    dynamic_slice x0 -> x16, local copies, waits for them, and re-layouts: none -> 37.8 us  [pick(): lax.dynamic_index_in_dim(arr, side, dim, keepdims=False)]
  transfers between devices with their start and end apart: 8 -> 48, of which waited for: 6 -> 32; matrix products, arithmetic and copies ran while one was open for 9% -> 26% of each run, Pallas kernels for 0% -> 0%
where the time goes in v2:
time: 1910 us
  waiting for transfers between devices  831 us (44%)
  matrix products  754 us (39%)
  local copies, waits for them, and re-layouts  142 us (7%)
  other arithmetic  123 us (6%)
  starting transfers between devices  44.2 us (2%)
    ppermute x40, waiting for transfers between devices, swap(): return lax.ppermute(arr, 'tp', [(i, i ^ bit) for i in range(tp_size)])  509 us
    all_gather x4, waiting for transfers between devices, device_fn(): zs.append(lax.all_gather(normed, 'tp', axis=0, tiled=True))  279 us
    dot_general x4, matrix products, device_fn(): jnp.einsum('sf,fd->sd', gated_act, w_down[layer], preferred_element_type=...  144 us
    dot_general x4, matrix products, device_fn(): jnp.einsum('sd,df->sf', zs[b], w_up[layer], preferred_element_type=jnp.fl...  144 us
    dot_general x4, matrix products, device_fn(): jnp.einsum('sd,df->sf', zs[b], w_gate[layer], preferred_element_type=jnp....  137 us
    sub x4, matrix products, attend(): prob_mat = jax.nn.softmax(scores, axis=-1).astype(jnp.bfloat16)  129 us
    dot_general x4, matrix products, attend(): jnp.einsum('kgqs,skd->qkgd', prob_mat, v_all, preferred_element_type=jnp....  98.4 us
    squeeze x32, local copies, waits for them, and re-layouts, pick(): lax.dynamic_index_in_dim(arr, side, dim, keepdims=False)  72.6 us
  transfers between devices with their start and end apart: 48, of which 32 were waited for; matrix products, arithmetic and copies ran while one was open for 26% of the time, Pallas kernels for 0%

profile of v2, /device:TPU:0, one launch (start us, length us, event | category | flops | bytes accessed | tf_op | source)
XLA Modules:
  0.0 1909.1 jit_solution(12293604764807804279)
XLA Ops:
  74.9 32.4 %fusion.232 = (f32[4,7,192]{2,1,0:T(8,128)S(1)}, f32[4,7,192,3072]{3,2,1,0:T(8,128)}) fusion(pred[192,3072]{1,0:T(8,128)(4,1)S(1)} %get-tuple-element.85, bf16[3072,8,128]{2,0,1:T(8,128)(2,1)} %all-gather.9.cloned.1.call-done, bf16[192,4,7,64]{3,0,2,1:T(8,128)(2,1)} %bitcast.542, bf16[192,4,7,64]{3,0,2,1:T(8,128)(2,1)} %bitcast.541), kind=kOutput, calls=%fused_computation.382 | convolution fusion | flops 4296674304 | bytes 72569856 | tf_op jit(solution)/shard_map/sub | solution.py:38
  146.6 93.2 %all-gather.11.cloned.1.call-done = bf16[3072,3584]{1,0:T(8,128)(2,1)} async-done(((bf16[192,3584]{1,0:T(8,128)(2,1)}), bf16[3072,3584]{1,0:T(8,128)(2,1)}) %all-gather.11.cloned.1.call-update) | async-done | bytes 22020112 | tf_op jit(solution)/shard_map/all_gather | solution.py:106
  239.7 34.1 %fusion.74 = f32[3072,1184]{0,1:T(8,128)} fusion(bf16[3072,3584]{1,0:T(8,128)(2,1)} %all-gather.11.cloned.1.call-done, bf16[2,3584,1184]{1,2,0:T(8,128)(2,1)} %param.20), kind=kOutput, calls=%fused_computation.98 | convolution fusion | flops 26071793664 | bytes 45056000 | tf_op jit(solution)/shard_map/sd,df->sf/dot_general | solution.py:108
  273.9 35.9 %fusion.56 = bf16[3072,1184]{0,1:T(8,128)(2,1)} fusion(bf16[3072,3584]{1,0:T(8,128)(2,1)} %all-gather.11.cloned.1.call-done, f32[3072,1184]{0,1:T(8,128)} %fusion.74, bf16[2,3584,1184]{1,2,0:T(8,128)(2,1)} %param.21), kind=kOutput, calls=%fused_computation.72 | convolution fusion | flops 26093617152 | bytes 52330496 | tf_op jit(solution)/shard_map/sd,df->sf/dot_general | solution.py:109
  309.8 36.3 %convolution_convert_fusion.3 = bf16[3072,3584]{1,0:T(8,128)(2,1)} fusion(bf16[3072,1184]{0,1:T(8,128)(2,1)} %fusion.56, bf16[2,1184,3584]{2,1,0:T(8,128)(2,1)} %param.22), kind=kOutput, calls=%fused_computation.59 | convolution fusion | flops 26082803712 | bytes 37781504 | tf_op jit(solution)/shard_map/sf,fd->sd/dot_general | solution.py:111
  411.6 66.0 %collective-permute-done.1 = f32[2,2,64,3584]{3,2,0,1:T(8,128)} collective-permute-done((f32[2,2,64,3584]{3,2,0,1:T(8,128)}, f32[2,2,64,3584]{3,2,0,1:T(8,128)}, u32[]{:S(2)}, u32[]{:S(2)}) %collective-permute-start.1) | collective-permute-done | bytes 3670048 | tf_op jit(solution)/shard_map/ppermute | solution.py:48
  490.7 32.4 %collective-permute-done.2 = f32[2,64,3584]{2,1,0:T(8,128)S(1)} collective-permute-done((f32[2,64,3584]{2,1,0:T(8,128)}, f32[2,64,3584]{2,1,0:T(8,128)S(1)}, u32[]{:S(2)}, u32[]{:S(2)}) %collective-permute-start.2) | collective-permute-done | bytes 1835040 | tf_op jit(solution)/shard_map/ppermute | solution.py:48
  597.4 32.4 %fusion.234 = (f32[4,7,192]{2,1,0:T(8,128)S(1)}, f32[4,7,192,3072]{3,2,1,0:T(8,128)}) fusion(pred[192,3072]{1,0:T(8,128)(4,1)S(1)} %copy-done.41, bf16[3072,8,128]{2,0,1:T(8,128)(2,1)} %all-gather.17.cloned.1.call-done, bf16[192,4,7,64]{3,0,2,1:T(8,128)(2,1)} %bitcast.543, bf16[192,4,7,64]{3,0,2,1:T(8,128)(2,1)} %bitcast.544), kind=kOutput, calls=%fused_computation.384 | convolution fusion | flops 4296674304 | bytes 72569856 | tf_op jit(solution)/shard_map/sub | solution.py:38
  669.2 93.2 %all-gather.19.cloned.1.call-done = bf16[3072,3584]{1,0:T(8,128)(2,1)} async-done(((bf16[192,3584]{1,0:T(8,128)(2,1)}), bf16[3072,3584]{1,0:T(8,128)(2,1)}) %all-gather.19.cloned.1.call-update) | async-done | bytes 22020112 | tf_op jit(solution)/shard_map/all_gather | solution.py:106
  762.4 34.1 %fusion.72 = f32[3072,1184]{0,1:T(8,128)} fusion(bf16[3072,3584]{1,0:T(8,128)(2,1)} %all-gather.19.cloned.1.call-done, bf16[2,3584,1184]{1,2,0:T(8,128)(2,1)} %param.20), kind=kOutput, calls=%fused_computation.96 | convolution fusion | flops 26071793664 | bytes 45056000 | tf_op jit(solution)/shard_map/sd,df->sf/dot_general | solution.py:108
  796.5 35.9 %fusion.58 = bf16[3072,1184]{0,1:T(8,128)(2,1)} fusion(bf16[3072,3584]{1,0:T(8,128)(2,1)} %all-gather.19.cloned.1.call-done, f32[3072,1184]{0,1:T(8,128)} %fusion.72, bf16[2,3584,1184]{1,2,0:T(8,128)(2,1)} %param.21), kind=kOutput, calls=%fused_computation.74 | convolution fusion | flops 26093617152 | bytes 52330496 | tf_op jit(solution)/shard_map/sd,df->sf/dot_general | solution.py:109
  832.5 36.1 %convolution_convert_fusion.1 = bf16[3072,3584]{1,0:T(8,128)(2,1)} fusion(bf16[3072,1184]{0,1:T(8,128)(2,1)} %fusion.58, bf16[2,1184,3584]{2,1,0:T(8,128)(2,1)} %param.22), kind=kOutput, calls=%fused_computation.57 | convolution fusion | flops 26082803712 | bytes 37781504 | tf_op jit(solution)/shard_map/sf,fd->sd/dot_general | solution.py:111
  927.5 86.0 %collective-permute-done.21 = f32[2,2,64,3584]{3,2,0,1:T(8,128)} collective-permute-done((f32[2,2,64,3584]{3,2,0,1:T(8,128)}, f32[2,2,64,3584]{3,2,0,1:T(8,128)}, u32[]{:S(2)}, u32[]{:S(2)}) %collective-permute-start.21) | collective-permute-done | bytes 3670048 | tf_op jit(solution)/shard_map/ppermute | solution.py:48
  1096.3 31.5 %fusion.233 = (f32[4,7,192]{2,1,0:T(8,128)}, f32[4,7,192,3072]{3,2,1,0:T(8,128)}) fusion(pred[192,3072]{1,0:T(8,128)(4,1)S(1)} %copy-done.44, bf16[3072,8,128]{2,0,1:T(8,128)(2,1)} %all-gather.13.cloned.1.call-done, bf16[192,4,7,64]{3,0,2,1:T(8,128)(2,1)S(1)} %bitcast.540, bf16[192,4,7,64]{3,0,2,1:T(8,128)(2,1)S(1)} %bitcast.539), kind=kOutput, calls=%fused_computation.383 | convolution fusion | flops 4296674304 | bytes 71193600 | tf_op jit(solution)/shard_map/sub | solution.py:38
  1178.7 32.5 %fusion.235 = (f32[4,7,192]{2,1,0:T(8,128)S(1)}, f32[4,7,192,3072]{3,2,1,0:T(8,128)}) fusion(pred[192,3072]{1,0:T(8,128)(4,1)S(1)} %copy-done.42, bf16[3072,8,128]{2,0,1:T(8,128)(2,1)} %all-gather.21.cloned.1.call-done, bf16[192,4,7,64]{3,0,2,1:T(8,128)(2,1)} %bitcast.546, bf16[192,4,7,64]{3,0,2,1:T(8,128)(2,1)} %bitcast.545), kind=kOutput, calls=%fused_computation.385 | convolution fusion | flops 4296674304 | bytes 72569856 | tf_op jit(solution)/shard_map/sub | solution.py:38
  1251.0 92.4 %all-gather.23.cloned.1.call-done = bf16[3072,3584]{1,0:T(8,128)(2,1)} async-done(((bf16[192,3584]{1,0:T(8,128)(2,1)}), bf16[3072,3584]{1,0:T(8,128)(2,1)}) %all-gather.23.cloned.1.call-update) | async-done | bytes 22020112 | tf_op jit(solution)/shard_map/all_gather | solution.py:106
  1343.4 34.1 %fusion.64 = f32[3072,1184]{0,1:T(8,128)} fusion(bf16[3072,3584]{1,0:T(8,128)(2,1)} %all-gather.23.cloned.1.call-done, bf16[2,3584,1184]{1,2,0:T(8,128)(2,1)} %param.20), kind=kOutput, calls=%fused_computation.88 | convolution fusion | flops 26071793664 | bytes 45056000 | tf_op jit(solution)/shard_map/sd,df->sf/dot_general | solution.py:108
  1377.5 35.9 %fusion.59 = bf16[3072,1184]{0,1:T(8,128)(2,1)} fusion(bf16[3072,3584]{1,0:T(8,128)(2,1)} %all-gather.23.cloned.1.call-done, f32[3072,1184]{0,1:T(8,128)} %fusion.64, bf16[2,3584,1184]{1,2,0:T(8,128)(2,1)} %param.21), kind=kOutput, calls=%fused_computation.75 | convolution fusion | flops 26093617152 | bytes 52330496 | tf_op jit(solution)/shard_map/sd,df->sf/dot_general | solution.py:109
  1413.4 36.2 %convolution_convert_fusion = bf16[3072,3584]{1,0:T(8,128)(2,1)} fusion(bf16[3072,1184]{0,1:T(8,128)(2,1)} %fusion.59, bf16[2,1184,3584]{2,1,0:T(8,128)(2,1)} %param.22), kind=kOutput, calls=%fused_computation.56 | convolution fusion | flops 26082803712 | bytes 37781504 | tf_op jit(solution)/shard_map/sf,fd->sd/dot_general | solution.py:111
  1465.3 34.1 %fusion.66 = f32[3072,1184]{0,1:T(8,128)} fusion(bf16[3072,3584]{1,0:T(8,128)(2,1)} %all-gather.15.cloned.1.call-done, bf16[2,3584,1184]{1,2,0:T(8,128)(2,1)} %param.20), kind=kOutput, calls=%fused_computation.90 | convolution fusion | flops 26071793664 | bytes 45056000 | tf_op jit(solution)/shard_map/sd,df->sf/dot_general | solution.py:108
  1499.4 36.0 %fusion.57 = bf16[3072,1184]{0,1:T(8,128)(2,1)} fusion(bf16[3072,3584]{1,0:T(8,128)(2,1)} %all-gather.15.cloned.1.call-done, f32[3072,1184]{0,1:T(8,128)} %fusion.66, bf16[2,3584,1184]{1,2,0:T(8,128)(2,1)} %param.21), kind=kOutput, calls=%fused_computation.73 | convolution fusion | flops 26093617152 | bytes 52330496 | tf_op jit(solution)/shard_map/sd,df->sf/dot_general | solution.py:109
  1535.4 35.9 %convolution_convert_fusion.2 = bf16[3072,3584]{1,0:T(8,128)(2,1)} fusion(bf16[3072,1184]{0,1:T(8,128)(2,1)} %fusion.57, bf16[2,1184,3584]{2,1,0:T(8,128)(2,1)} %param.22), kind=kOutput, calls=%fused_computation.58 | convolution fusion | flops 26082803712 | bytes 37781504 | tf_op jit(solution)/shard_map/sf,fd->sd/dot_general | solution.py:111
  1645.1 44.8 %collective-permute-done.31 = f32[2,2,64,3584]{3,2,0,1:T(8,128)} collective-permute-done((f32[2,2,64,3584]{3,2,0,1:T(8,128)}, f32[2,2,64,3584]{3,2,0,1:T(8,128)}, u32[]{:S(2)}, u32[]{:S(2)}) %collective-permute-start.31) | collective-permute-done | bytes 3670048 | tf_op jit(solution)/shard_map/ppermute | solution.py:48
  1706.6 61.2 %collective-permute-done.11 = f32[2,2,64,3584]{3,2,0,1:T(8,128)} collective-permute-done((f32[2,2,64,3584]{3,2,0,1:T(8,128)}, f32[2,2,64,3584]{3,2,0,1:T(8,128)}, u32[]{:S(2)}, u32[]{:S(2)}) %collective-permute-start.11) | collective-permute-done | bytes 3670048 | tf_op jit(solution)/shard_map/ppermute | solution.py:48
  (388 shorter events, 771.6 us)
Async XLA Ops:
  30.1 209.6 %all-gather.11.cloned.1.call-start = ((), (), s32[]{:S(2)}) async-start(), calls=%async_computation.1 | async-start | bytes 23396352 | tf_op jit(solution)/shard_map/all_gather | solution.py:106
  146.5 450.9 %all-gather.17.cloned.1.call-start = ((), (), s32[]{:S(2)}) async-start(), calls=%async_computation.4 | async-start | bytes 6684672 | tf_op jit(solution)/shard_map/all_gather | solution.py:97
  396.0 81.5 %collective-permute-start.1 = (f32[2,2,64,3584]{3,2,0,1:T(8,128)}, f32[2,2,64,3584]{3,2,0,1:T(8,128)}, u32[]{:S(2)}, u32[]{:S(2)}) collective-permute-start(f32[2,2,64,3584]{3,2,0,1:T(8,128)} %bitcast.525), channel_id=1, source_target_pairs={{0,2},{1,3},{2,0},{3,1},{4,6},{5,7},{6,4},{7,5},{8,10},{9,11},{10,... | collective-permute-start | bytes 11010056 | tf_op jit(solution)/shard_map/ppermute | solution.py:48
  401.8 81.3 %collective-permute-start.4 = (f32[2,2,64,3584]{3,2,1,0:T(8,128)}, f32[2,2,64,3584]{3,2,1,0:T(8,128)}, u32[]{:S(2)}, u32[]{:S(2)}) collective-permute-start(f32[2,2,64,3584]{3,2,1,0:T(8,128)} %dynamic-slice_bitcast_fusion.11), channel_id=1, source_target_pairs={{0,4},{1,5},{2,6},{3,7},{4,0},{5,1},{6,2},{7,3},{8,12},{9,13},{10,... | collective-permute-start | bytes 11010056 | tf_op jit(solution)/shard_map/ppermute | solution.py:48
  408.0 82.1 %collective-permute-start.7 = (f32[2,2,64,3584]{3,2,0,1:T(8,128)S(1)}, f32[2,2,64,3584]{3,2,0,1:T(8,128)S(1)}, u32[]{:S(2)}, u32[]{:S(2)}) collective-permute-start(f32[2,2,64,3584]{3,2,0,1:T(8,128)S(1)} %bitcast.538), channel_id=1, source_target_pairs={{0,8},{1,9},{2,10},{3,11},{4,12},{5,13},{6,14},{7,15},{8,0},{9,1},... | collective-permute-start | bytes 11010056 | tf_op jit(solution)/shard_map/ppermute | solution.py:48
  555.8 206.6 %all-gather.19.cloned.1.call-start = ((), (), s32[]{:S(2)}) async-start(), calls=%async_computation.5 | async-start | bytes 23396352 | tf_op jit(solution)/shard_map/all_gather | solution.py:106
  669.2 427.1 %all-gather.13.cloned.1.call-start = ((), (), s32[]{:S(2)}) async-start(), calls=%async_computation.2 | async-start | bytes 6684672 | tf_op jit(solution)/shard_map/all_gather | solution.py:97
  912.3 101.2 %collective-permute-start.21 = (f32[2,2,64,3584]{3,2,0,1:T(8,128)}, f32[2,2,64,3584]{3,2,0,1:T(8,128)}, u32[]{:S(2)}, u32[]{:S(2)}) collective-permute-start(f32[2,2,64,3584]{3,2,0,1:T(8,128)} %bitcast.521), channel_id=1, source_target_pairs={{0,2},{1,3},{2,0},{3,1},{4,6},{5,7},{6,4},{7,5},{8,10},{9,11},{10,... | collective-permute-start | bytes 11010056 | tf_op jit(solution)/shard_map/ppermute | solution.py:48
  916.8 102.1 %collective-permute-start.24 = (f32[2,2,64,3584]{3,2,1,0:T(8,128)}, f32[2,2,64,3584]{3,2,1,0:T(8,128)}, u32[]{:S(2)}, u32[]{:S(2)}) collective-permute-start(f32[2,2,64,3584]{3,2,1,0:T(8,128)} %dynamic-slice_bitcast_fusion.9), channel_id=1, source_target_pairs={{0,4},{1,5},{2,6},{3,7},{4,0},{5,1},{6,2},{7,3},{8,12},{9,13},{10,... | collective-permute-start | bytes 11010056 | tf_op jit(solution)/shard_map/ppermute | solution.py:48
  923.5 101.9 %collective-permute-start.27 = (f32[2,2,64,3584]{3,2,0,1:T(8,128)}, f32[2,2,64,3584]{3,2,0,1:T(8,128)}, u32[]{:S(2)}, u32[]{:S(2)}) collective-permute-start(f32[2,2,64,3584]{3,2,0,1:T(8,128)} %bitcast.520), channel_id=1, source_target_pairs={{0,8},{1,9},{2,10},{3,11},{4,12},{5,13},{6,14},{7,15},{8,0},{9,1},... | collective-permute-start | bytes 11010056 | tf_op jit(solution)/shard_map/ppermute | solution.py:48
  927.0 251.7 %all-gather.21.cloned.1.call-start = ((), (), s32[]{:S(2)}) async-start(), calls=%async_computation.6 | async-start | bytes 6684672 | tf_op jit(solution)/shard_map/all_gather | solution.py:97
  1096.2 247.2 %all-gather.23.cloned.1.call-start = ((), (), s32[]{:S(2)}) async-start(), calls=%async_computation.7 | async-start | bytes 23396352 | tf_op jit(solution)/shard_map/all_gather | solution.py:106
  1250.2 215.1 %all-gather.15.cloned.1.call-start = ((), (), s32[]{:S(2)}) async-start(), calls=%async_computation.3 | async-start | bytes 23396352 | tf_op jit(solution)/shard_map/all_gather | solution.py:106
  1465.0 118.9 %collective-permute-start.30 = (bf16[2,2,2,192,3584]{4,3,2,1,0:T(8,128)(2,1)}, bf16[2,2,2,192,3584]{4,3,2,1,0:T(8,128)(2,1)}, u32[]{:S(2)}, u32[]{:S(2)}) collective-permute-start(bf16[2,2,2,192,3584]{4,3,2,1,0:T(8,128)(2,1)} %get-tuple-element.33), channel_id=1, source_target_pairs={{0,1},{1,0},{2,3},{3,2},{4,5},{5,4},{6,7},{7,6},{8,9},{9,8},{10,11... | collective-permute-start | bytes 33030152 | tf_op jit(solution)/shard_map/ppermute | solution.py:48
  1607.6 82.2 %collective-permute-start.31 = (f32[2,2,64,3584]{3,2,0,1:T(8,128)}, f32[2,2,64,3584]{3,2,0,1:T(8,128)}, u32[]{:S(2)}, u32[]{:S(2)}) collective-permute-start(f32[2,2,64,3584]{3,2,0,1:T(8,128)} %bitcast.519), channel_id=1, source_target_pairs={{0,2},{1,3},{2,0},{3,1},{4,6},{5,7},{6,4},{7,5},{8,10},{9,11},{10,... | collective-permute-start | bytes 11010056 | tf_op jit(solution)/shard_map/ppermute | solution.py:48
  1612.1 83.7 %collective-permute-start.34 = (f32[2,2,64,3584]{3,2,1,0:T(8,128)}, f32[2,2,64,3584]{3,2,1,0:T(8,128)}, u32[]{:S(2)}, u32[]{:S(2)}) collective-permute-start(f32[2,2,64,3584]{3,2,1,0:T(8,128)} %dynamic-slice_bitcast_fusion.8), channel_id=1, source_target_pairs={{0,4},{1,5},{2,6},{3,7},{4,0},{5,1},{6,2},{7,3},{8,12},{9,13},{10,... | collective-permute-start | bytes 11010056 | tf_op jit(solution)/shard_map/ppermute | solution.py:48
  1618.7 82.6 %collective-permute-start.37 = (f32[2,2,64,3584]{3,2,0,1:T(8,128)}, f32[2,2,64,3584]{3,2,0,1:T(8,128)}, u32[]{:S(2)}, u32[]{:S(2)}) collective-permute-start(f32[2,2,64,3584]{3,2,0,1:T(8,128)} %bitcast.518), channel_id=1, source_target_pairs={{0,8},{1,9},{2,10},{3,11},{4,12},{5,13},{6,14},{7,15},{8,0},{9,1},... | collective-permute-start | bytes 11010056 | tf_op jit(solution)/shard_map/ppermute | solution.py:48
  1635.8 132.0 %collective-permute-start.11 = (f32[2,2,64,3584]{3,2,0,1:T(8,128)}, f32[2,2,64,3584]{3,2,0,1:T(8,128)}, u32[]{:S(2)}, u32[]{:S(2)}) collective-permute-start(f32[2,2,64,3584]{3,2,0,1:T(8,128)} %bitcast.523), channel_id=1, source_target_pairs={{0,2},{1,3},{2,0},{3,1},{4,6},{5,7},{6,4},{7,5},{8,10},{9,11},{10,... | collective-permute-start | bytes 11010056 | tf_op jit(solution)/shard_map/ppermute | solution.py:48
  1640.2 132.9 %collective-permute-start.14 = (f32[2,2,64,3584]{3,2,1,0:T(8,128)}, f32[2,2,64,3584]{3,2,1,0:T(8,128)}, u32[]{:S(2)}, u32[]{:S(2)}) collective-permute-start(f32[2,2,64,3584]{3,2,1,0:T(8,128)} %dynamic-slice_bitcast_fusion.10), channel_id=1, source_target_pairs={{0,4},{1,5},{2,6},{3,7},{4,0},{5,1},{6,2},{7,3},{8,12},{9,13},{10,... | collective-permute-start | bytes 11010056 | tf_op jit(solution)/shard_map/ppermute | solution.py:48
  1689.8 89.7 %collective-permute-start.17 = (f32[2,2,64,3584]{3,2,0,1:T(8,128)}, f32[2,2,64,3584]{3,2,0,1:T(8,128)}, u32[]{:S(2)}, u32[]{:S(2)}) collective-permute-start(f32[2,2,64,3584]{3,2,0,1:T(8,128)} %bitcast.522), channel_id=1, source_target_pairs={{0,8},{1,9},{2,10},{3,11},{4,12},{5,13},{6,14},{7,15},{8,0},{9,1},... | collective-permute-start | bytes 11010056 | tf_op jit(solution)/shard_map/ppermute | solution.py:48
  1695.8 116.5 %collective-permute-start.32 = (f32[2,64,3584]{2,1,0:T(8,128)}, f32[2,64,3584]{2,1,0:T(8,128)}, u32[]{:S(2)}, u32[]{:S(2)}) collective-permute-start(f32[2,64,3584]{2,1,0:T(8,128)} %dynamic-slice_bitcast_fusion.14), channel_id=1, source_target_pairs={{0,4},{1,5},{2,6},{3,7},{4,0},{5,1},{6,2},{7,3},{8,12},{9,13},{10,... | collective-permute-start | bytes 5505032 | tf_op jit(solution)/shard_map/ppermute | solution.py:48
  1701.3 117.6 %collective-permute-start.35 = (f32[2,64,3584]{2,1,0:T(8,128)}, f32[2,64,3584]{2,1,0:T(8,128)}, u32[]{:S(2)}, u32[]{:S(2)}) collective-permute-start(f32[2,64,3584]{2,1,0:T(8,128)} %dynamic-slice_bitcast_fusion.13), channel_id=1, source_target_pairs={{0,8},{1,9},{2,10},{3,11},{4,12},{5,13},{6,14},{7,15},{8,0},{9,1},... | collective-permute-start | bytes 5505032 | tf_op jit(solution)/shard_map/ppermute | solution.py:48
  1773.0 77.9 %collective-permute-start.12 = (f32[2,64,3584]{2,1,0:T(8,128)}, f32[2,64,3584]{2,1,0:T(8,128)S(1)}, u32[]{:S(2)}, u32[]{:S(2)}) collective-permute-start(f32[2,64,3584]{2,1,0:T(8,128)} %dynamic-slice_bitcast_fusion.20), channel_id=1, source_target_pairs={{0,4},{1,5},{2,6},{3,7},{4,0},{5,1},{6,2},{7,3},{8,12},{9,13},{10,... | collective-permute-start | bytes 5505032 | tf_op jit(solution)/shard_map/ppermute | solution.py:48
  1779.5 78.6 %collective-permute-start.15 = (f32[2,64,3584]{2,1,0:T(8,128)}, f32[2,64,3584]{2,1,0:T(8,128)S(1)}, u32[]{:S(2)}, u32[]{:S(2)}) collective-permute-start(f32[2,64,3584]{2,1,0:T(8,128)} %dynamic-slice_bitcast_fusion.19), channel_id=1, source_target_pairs={{0,8},{1,9},{2,10},{3,11},{4,12},{5,13},{6,14},{7,15},{8,0},{9,1},... | collective-permute-start | bytes 5505032 | tf_op jit(solution)/shard_map/ppermute | solution.py:48
  (94 other events, 1820.6 us)
Sparse Core Ops, SparseCore 0:
  30.3 44.5 all-gather.8
  146.6 93.0 all-gather.10
  555.9 41.4 all-gather.16
  669.3 93.0 all-gather.18
  927.1 62.5 all-gather.12
  1096.3 41.7 all-gather.20
  1250.3 93.0 all-gather.22
  1345.6 93.0 all-gather.14
